TPU v7x, 32 devices: a whole 2x2x4 slice. The times are simulated.
32 devices in a mesh: clip: 4 (over x, core), seq: 2 (over y), head: 4 (over z).
Axes of the slice: x: 2, y: 2, z: 4, core: 2. Of those that a mesh axis runs over, the one named last changes fastest.
Arguments:
- inputs: bfloat16 [4, 1500, 768], P('clip', 'seq'), may hold values from -6 to 6
- gain_one: bfloat16 [768], P(('clip', 'seq')), may hold values from 0.25 to 1.75
- shift_one: bfloat16 [768], P(('clip', 'seq')), may hold values from -1.75 to 1.75
- w_query: bfloat16 [768, 768], P(('clip', 'seq'), 'head'), may hold values from -0.21875 to 0.21875
- b_query: bfloat16 [768], P('head'), may hold values from -3 to 3
- w_key: bfloat16 [768, 768], P(('clip', 'seq'), 'head'), may hold values from -0.21875 to 0.21875
- w_value: bfloat16 [768, 768], P(('clip', 'seq'), 'head'), may hold values from -0.21875 to 0.21875
- b_value: bfloat16 [768], P('head'), may hold values from -0.3125 to 0.3125
- w_out: bfloat16 [768, 768], P('head', ('clip', 'seq')), may hold values from -3.5 to 3.5
- b_out: bfloat16 [768], P(('clip', 'seq')), may hold values from -3 to 3
- gain_two: bfloat16 [768], P(('clip', 'seq')), may hold values from 0.25 to 1.75
- shift_two: bfloat16 [768], P(('clip', 'seq')), may hold values from -1.75 to 1.75
- w_fc_one: bfloat16 [768, 3072], P(('clip', 'seq'), 'head'), may hold values from -0.21875 to 0.21875
- b_fc_one: bfloat16 [3072], P('head'), may hold values from -3 to 3
- w_fc_two: bfloat16 [3072, 768], P('head', ('clip', 'seq')), may hold values from -0.3125 to 0.3125
- b_fc_two: bfloat16 [768], P(('clip', 'seq')), may hold values from -3 to 3
- cotangent: bfloat16 [4, 1500, 768], P('clip', 'seq'), may hold values from -6 to 6
Outputs:
- outputs: bfloat16 [4, 1500, 768], P('clip', 'seq')
- input_gradient: float32 [4, 1500, 768], P('clip', 'seq')
- first_gain_gradient: float32 [768], P(('clip', 'seq'))
- grad_shift_one: float32 [768], P(('clip', 'seq'))
- grad_w_query: float32 [768, 768], P(('clip', 'seq'), 'head')
- grad_b_query: float32 [768], P('head')
- grad_w_key: float32 [768, 768], P(('clip', 'seq'), 'head')
- grad_w_value: float32 [768, 768], P(('clip', 'seq'), 'head')
- grad_b_value: float32 [768], P('head')
- grad_w_out: float32 [768, 768], P('head', ('clip', 'seq'))
- grad_b_out: float32 [768], P(('clip', 'seq'))
- second_gain_gradient: float32 [768], P(('clip', 'seq'))
- grad_shift_two: float32 [768], P(('clip', 'seq'))
- grad_w_fc_one: float32 [768, 3072], P(('clip', 'seq'), 'head')
- grad_b_fc_one: float32 [3072], P('head')
- grad_w_fc_two: float32 [3072, 768], P('head', ('clip', 'seq'))
- grad_b_fc_two: float32 [768], P(('clip', 'seq'))
All inputs are finite; a program needn't handle non-finite values.
Results may differ from a plain program's by a relative error of at most 0.012.
Values may be sent and summed in bfloat16 or wider, within the bound.
A program may use at most 128 MiB of HBM per device.

v0:
```python
from functools import partial
import jax
import jax.numpy as jnp
from jax import lax
from jax.sharding import PartitionSpec as P

HEAD_DIM = 64
eps = 1e-05


def layer_norm_forward(values, norm_gain, norm_shift):
    row_mean = jnp.mean(values, axis=-1, keepdims=True)
    centered_values = values - row_mean
    spread = jnp.mean(centered_values * centered_values, axis=-1, keepdims=True)
    inverse_deviation = lax.rsqrt(spread + eps)
    standardized = centered_values * inverse_deviation
    return (standardized * norm_gain + norm_shift, standardized, inverse_deviation)


def layer_norm_backward(output_gradient, standardized, inverse_deviation, norm_gain):
    scaled_rows = output_gradient * norm_gain
    first_row_mean = jnp.mean(scaled_rows, axis=-1, keepdims=True)
    second_row_mean = jnp.mean(scaled_rows * standardized, axis=-1, keepdims=True)
    return inverse_deviation * (scaled_rows - first_row_mean - standardized * second_row_mean)


def fetch_weights(
    gain_one,
    shift_one,
    w_query,
    w_key,
    w_value,
    b_out,
    gain_two,
    shift_two,
    w_fc_one,
    b_fc_two,
    w_out,
    w_fc_two,
):
    rows = (
        lax.all_gather(gain_one, ("clip", "seq"), axis=0, tiled=True),
        lax.all_gather(shift_one, ("clip", "seq"), axis=0, tiled=True),
        lax.all_gather(w_query, ("clip", "seq"), axis=0, tiled=True),
        lax.all_gather(w_key, ("clip", "seq"), axis=0, tiled=True),
        lax.all_gather(w_value, ("clip", "seq"), axis=0, tiled=True),
        lax.all_gather(b_out, ("clip", "seq"), axis=0, tiled=True),
        lax.all_gather(gain_two, ("clip", "seq"), axis=0, tiled=True),
        lax.all_gather(shift_two, ("clip", "seq"), axis=0, tiled=True),
        lax.all_gather(w_fc_one, ("clip", "seq"), axis=0, tiled=True),
        lax.all_gather(b_fc_two, ("clip", "seq"), axis=0, tiled=True),
    )
    columns = (
        lax.all_gather(w_out, ("clip", "seq"), axis=1, tiled=True),
        lax.all_gather(w_fc_two, ("clip", "seq"), axis=1, tiled=True),
    )
    return (rows, columns)


def head_total(partial_sum):
    return lax.psum(partial_sum, "head")


def on_device(
    inputs,
    gain_one,
    shift_one,
    w_query,
    b_query,
    w_key,
    w_value,
    b_value,
    w_out,
    b_out,
    gain_two,
    shift_two,
    w_fc_one,
    b_fc_one,
    w_fc_two,
    b_fc_two,
    cotangent,
):
    clips, frames, width = inputs.shape
    local = w_query.shape[1]
    heads = local // HEAD_DIM
    scale = HEAD_DIM ** (-0.5)
    gathered_rows = jnp.float32
    count = clips * frames
    rows, columns = fetch_weights(
        gain_one,
        shift_one,
        w_query,
        w_key,
        w_value,
        b_out,
        gain_two,
        shift_two,
        w_fc_one,
        b_fc_two,
        w_out,
        w_fc_two,
    )
    (
        full_gain_one,
        gathered_first_shift,
        full_query,
        full_key,
        full_value,
        full_b_out,
        full_gain_two,
        gathered_second_shift,
        full_fc_one,
        full_b_fc_two,
    ) = rows
    full_out, full_fc_two = columns
    token_rows = inputs.astype(gathered_rows).reshape(count, width)
    first_norm_gain = full_gain_one.astype(gathered_rows)
    second_norm_gain = full_gain_two.astype(gathered_rows)
    normalized_gathered, first_standardized, first_inverse_deviation = layer_norm_forward(
        token_rows, first_norm_gain, gathered_first_shift.astype(gathered_rows)
    )
    normed_one = normalized_gathered.astype(jnp.bfloat16)
    query = (
        jnp.dot(normed_one, full_query, preferred_element_type=gathered_rows)
        + b_query.astype(gathered_rows)
    ).astype(jnp.bfloat16)
    key = jnp.dot(normed_one, full_key, preferred_element_type=gathered_rows).astype(jnp.bfloat16)
    value = (
        jnp.dot(normed_one, full_value, preferred_element_type=gathered_rows)
        + b_value.astype(gathered_rows)
    ).astype(jnp.bfloat16)
    query_clips = query.reshape(clips, frames, local)
    key_all, value_all = (
        lax.all_gather(key.reshape(clips, frames, local), "seq", axis=1, tiled=True),
        lax.all_gather(value.reshape(clips, frames, local), "seq", axis=1, tiled=True),
    )

    def attend(block):
        query_block, key_block, value_block = block
        query_heads = query_block.reshape(frames, heads, HEAD_DIM)
        key_heads = key_block.reshape(-1, heads, HEAD_DIM)
        value_heads = value_block.reshape(-1, heads, HEAD_DIM)
        scores = (
            jnp.einsum("qhd,khd->hqk", query_heads, key_heads, preferred_element_type=gathered_rows)
            * scale
        )
        top = jnp.max(scores, axis=-1, keepdims=True)
        expo = jnp.exp(scores - top)
        total = jnp.sum(expo, axis=-1, keepdims=True)
        probs = (expo / total).astype(jnp.bfloat16)
        result = jnp.einsum(
            "hqk,khd->qhd", probs, value_heads, preferred_element_type=gathered_rows
        )
        return (result.reshape(frames, local).astype(jnp.bfloat16), (top + jnp.log(total))[..., 0])

    attended_clips, log_totals = lax.map(attend, (query_clips, key_all, value_all))
    attended = attended_clips.reshape(count, local)
    attn_terms = jnp.dot(attended, full_out, preferred_element_type=gathered_rows)
    middle_state = token_rows + head_total(attn_terms) + full_b_out.astype(gathered_rows)
    normalized_middle, second_standardized, second_inverse_deviation = layer_norm_forward(
        middle_state, second_norm_gain, gathered_second_shift.astype(gathered_rows)
    )
    normed_two = normalized_middle.astype(jnp.bfloat16)
    pre = jnp.dot(normed_two, full_fc_one, preferred_element_type=gathered_rows) + b_fc_one.astype(
        gathered_rows
    )
    act = jax.nn.gelu(pre, approximate=False).astype(jnp.bfloat16)
    ffn_terms = jnp.dot(act, full_fc_two, preferred_element_type=gathered_rows)
    outputs = (middle_state + head_total(ffn_terms) + full_b_fc_two.astype(gathered_rows)).astype(
        jnp.bfloat16
    )
    rows, columns = fetch_weights(
        gain_one,
        shift_one,
        w_query,
        w_key,
        w_value,
        b_out,
        gain_two,
        shift_two,
        w_fc_one,
        b_fc_two,
        w_out,
        w_fc_two,
    )
    (
        full_gain_one,
        gathered_first_shift,
        full_query,
        full_key,
        full_value,
        full_b_out,
        full_gain_two,
        gathered_second_shift,
        full_fc_one,
        full_b_fc_two,
    ) = rows
    full_out, full_fc_two = columns
    first_norm_gain = full_gain_one.astype(gathered_rows)
    second_norm_gain = full_gain_two.astype(gathered_rows)
    upstream_gradient = cotangent.astype(gathered_rows).reshape(count, width)
    grad_b_fc_two = jnp.sum(upstream_gradient, axis=0)
    grad_top_low = upstream_gradient.astype(jnp.bfloat16)
    grad_w_fc_two = jnp.einsum("tf,td->fd", act, grad_top_low, preferred_element_type=gathered_rows)
    grad_act = jnp.einsum(
        "td,fd->tf", grad_top_low, full_fc_two, preferred_element_type=gathered_rows
    )
    unused, gelu_back = jax.vjp(partial(jax.nn.gelu, approximate=False), pre)
    grad_pre = gelu_back(grad_act)[0].astype(jnp.bfloat16)
    grad_b_fc_one = jnp.sum(grad_pre.astype(gathered_rows), axis=0)
    grad_w_fc_one = jnp.einsum(
        "td,tf->df", normed_two, grad_pre, preferred_element_type=gathered_rows
    )
    normed_two_terms = jnp.einsum(
        "tf,df->td", grad_pre, full_fc_one, preferred_element_type=gathered_rows
    )
    second_normalized_gradient = head_total(normed_two_terms)
    middle_gradient = upstream_gradient + layer_norm_backward(
        second_normalized_gradient, second_standardized, second_inverse_deviation, second_norm_gain
    )
    grad_mid_low = middle_gradient.astype(jnp.bfloat16)
    second_gain_gradient = jnp.sum(second_normalized_gradient * second_standardized, axis=0)
    grad_shift_two = jnp.sum(second_normalized_gradient, axis=0)
    grad_b_out = jnp.sum(middle_gradient, axis=0)
    grad_w_out = jnp.einsum(
        "tj,td->jd", attended, grad_mid_low, preferred_element_type=gathered_rows
    )
    grad_attended = jnp.einsum(
        "td,jd->tj", grad_mid_low, full_out, preferred_element_type=gathered_rows
    ).astype(jnp.bfloat16)

    def attend_back(block):
        query_block, key_block, value_block, grad_block, log_block = block
        query_heads = query_block.reshape(frames, heads, HEAD_DIM)
        key_heads = key_block.reshape(-1, heads, HEAD_DIM)
        value_heads = value_block.reshape(-1, heads, HEAD_DIM)
        grad_heads = grad_block.reshape(frames, heads, HEAD_DIM)
        scores = (
            jnp.einsum("qhd,khd->hqk", query_heads, key_heads, preferred_element_type=gathered_rows)
            * scale
        )
        probs = jnp.exp(scores - log_block[..., None])
        grad_values = jnp.einsum(
            "hqk,qhd->khd",
            probs.astype(jnp.bfloat16),
            grad_heads,
            preferred_element_type=gathered_rows,
        )
        grad_probs = jnp.einsum(
            "qhd,khd->hqk", grad_heads, value_heads, preferred_element_type=gathered_rows
        )
        inner = jnp.sum(probs * grad_probs, axis=-1, keepdims=True)
        grad_scores = (probs * (grad_probs - inner)).astype(jnp.bfloat16)
        grad_queries = (
            jnp.einsum("hqk,khd->qhd", grad_scores, key_heads, preferred_element_type=gathered_rows)
            * scale
        )
        grad_keys = (
            jnp.einsum(
                "hqk,qhd->khd", grad_scores, query_heads, preferred_element_type=gathered_rows
            )
            * scale
        )
        return (
            grad_queries.reshape(frames, local).astype(jnp.bfloat16),
            grad_keys.reshape(-1, local),
            grad_values.reshape(-1, local),
        )

    grad_query_clips, grad_key_all, grad_value_all = lax.map(
        attend_back,
        (query_clips, key_all, value_all, grad_attended.reshape(clips, frames, local), log_totals),
    )
    grad_key_own, grad_value_own = (
        lax.psum_scatter(grad_key_all, "seq", scatter_dimension=1, tiled=True),
        lax.psum_scatter(grad_value_all, "seq", scatter_dimension=1, tiled=True),
    )
    grad_query = grad_query_clips.reshape(count, local)
    grad_key = grad_key_own.reshape(count, local).astype(jnp.bfloat16)
    grad_value = grad_value_own.reshape(count, local).astype(jnp.bfloat16)
    grad_b_query = jnp.sum(grad_query.astype(gathered_rows), axis=0)
    grad_b_value = jnp.sum(grad_value.astype(gathered_rows), axis=0)
    grad_w_query = jnp.einsum(
        "td,tj->dj", normed_one, grad_query, preferred_element_type=gathered_rows
    )
    grad_w_key = jnp.einsum("td,tj->dj", normed_one, grad_key, preferred_element_type=gathered_rows)
    grad_w_value = jnp.einsum(
        "td,tj->dj", normed_one, grad_value, preferred_element_type=gathered_rows
    )
    grad_normed_part = jnp.einsum(
        "tj,dj->td", grad_query, full_query, preferred_element_type=gathered_rows
    )
    grad_normed_part = grad_normed_part + jnp.einsum(
        "tj,dj->td", grad_key, full_key, preferred_element_type=gathered_rows
    )
    grad_normed_part = grad_normed_part + jnp.einsum(
        "tj,dj->td", grad_value, full_value, preferred_element_type=gathered_rows
    )
    first_normalized_gradient = head_total(grad_normed_part)
    first_gain_gradient = jnp.sum(first_normalized_gradient * first_standardized, axis=0)
    grad_shift_one = jnp.sum(first_normalized_gradient, axis=0)
    input_gradient = middle_gradient + layer_norm_backward(
        first_normalized_gradient, first_standardized, first_inverse_deviation, first_norm_gain
    )
    owned_rows = (
        lax.psum_scatter(first_gain_gradient, ("clip", "seq"), scatter_dimension=0, tiled=True),
        lax.psum_scatter(grad_shift_one, ("clip", "seq"), scatter_dimension=0, tiled=True),
        lax.psum_scatter(grad_w_query, ("clip", "seq"), scatter_dimension=0, tiled=True),
        lax.psum_scatter(grad_w_key, ("clip", "seq"), scatter_dimension=0, tiled=True),
        lax.psum_scatter(grad_w_value, ("clip", "seq"), scatter_dimension=0, tiled=True),
        lax.psum_scatter(grad_b_out, ("clip", "seq"), scatter_dimension=0, tiled=True),
        lax.psum_scatter(second_gain_gradient, ("clip", "seq"), scatter_dimension=0, tiled=True),
        lax.psum_scatter(grad_shift_two, ("clip", "seq"), scatter_dimension=0, tiled=True),
        lax.psum_scatter(grad_w_fc_one, ("clip", "seq"), scatter_dimension=0, tiled=True),
        lax.psum_scatter(grad_b_fc_two, ("clip", "seq"), scatter_dimension=0, tiled=True),
    )
    owned_columns = (
        lax.psum_scatter(grad_w_out, ("clip", "seq"), scatter_dimension=1, tiled=True),
        lax.psum_scatter(grad_w_fc_two, ("clip", "seq"), scatter_dimension=1, tiled=True),
    )
    bias_totals = lax.psum((grad_b_query, grad_b_value, grad_b_fc_one), ("clip", "seq"))
    return (
        outputs.reshape(clips, frames, width),
        input_gradient.reshape(clips, frames, width),
        owned_rows[0],
        owned_rows[1],
        owned_rows[2],
        bias_totals[0],
        owned_rows[3],
        owned_rows[4],
        bias_totals[1],
        owned_columns[0],
        owned_rows[5],
        owned_rows[6],
        owned_rows[7],
        owned_rows[8],
        bias_totals[2],
        owned_columns[1],
        owned_rows[9],
    )


def solution(mesh):
    return jax.shard_map(
        on_device,
        mesh=mesh,
        in_specs=(
            P("clip", "seq", None),
            P(("clip", "seq")),
            P(("clip", "seq")),
            P(("clip", "seq"), "head"),
            P("head"),
            P(("clip", "seq"), "head"),
            P(("clip", "seq"), "head"),
            P("head"),
            P("head", ("clip", "seq")),
            P(("clip", "seq")),
            P(("clip", "seq")),
            P(("clip", "seq")),
            P(("clip", "seq"), "head"),
            P("head"),
            P("head", ("clip", "seq")),
            P(("clip", "seq")),
            P("clip", "seq", None),
        ),
        out_specs=(
            P("clip", "seq", None),
            P("clip", "seq", None),
            P(("clip", "seq")),
            P(("clip", "seq")),
            P(("clip", "seq"), "head"),
            P("head"),
            P(("clip", "seq"), "head"),
            P(("clip", "seq"), "head"),
            P("head"),
            P("head", ("clip", "seq")),
            P(("clip", "seq")),
            P(("clip", "seq")),
            P(("clip", "seq")),
            P(("clip", "seq"), "head"),
            P("head"),
            P("head", ("clip", "seq")),
            P(("clip", "seq")),
        ),
        check_vma=False,
    )
```

profile of v0, /device:TPU:0, one launch (start us, length us, event | category | flops | bytes accessed | tf_op | source)
XLA Modules:
  0.0 687.4 jit_solution(10025798544051608802)
XLA Ops:
  15.1 25.7 %all-reduce.17 = (bf16[768]{0:T(1024)(128)(2,1)S(1)}, bf16[768]{0:T(1024)(128)(2,1)S(1)}, bf16[768]{0:T(1024)(128)(2,1)S(1)}, bf16[768]{0:T(1024)(128)(2,1)S(1)}...) all-reduce(bf16[768]{0:T(1024)(128)(2,1)S(1)} %dynamic-update-slice, ...), channel_id=1, replica_groups=mesh['clip'=4,'seq'=2,'head'=4] {'clip','seq'}, use_global_device_ids=true, to_apply=%add.1 | all-reduce | flops 4608 | bytes 18432
  44.1 15.9 %all_gather.55 = bf16[768,192]{1,0:T(8,128)(2,1)S(1)} all-gather(bf16[96,192]{1,0:T(8,128)(2,1)S(1)} %copy-done.26), channel_id=1, replica_groups=mesh['clip'=4,'seq'=2,'head'=4] {'clip','seq'}, dimensions={0}, use_global_device_ids=true | all-gather | bytes 331776 | tf_op jit(solution)/shard_map/all_gather | solution.py:45
  61.1 10.5 %all-gather.3 = bf16[2,750,192]{1,2,0:T(8,128)(2,1)S(1)} all-gather(bf16[1,750,192]{1,2,0:T(8,128)(2,1)S(1)} %fusion.39), channel_id=3, replica_groups=mesh['clip'=4,'seq'=2,'head'=4] {'seq'}, dimensions={0}, use_global_device_ids=true | all-gather | bytes 864000 | tf_op jit(solution)/shard_map/all_gather | solution.py:134
  75.3 15.6 %all_gather.54 = bf16[768,192]{1,0:T(8,128)(2,1)S(1)} all-gather(bf16[96,192]{1,0:T(8,128)(2,1)S(1)} %copy-done.27), channel_id=1, replica_groups=mesh['clip'=4,'seq'=2,'head'=4] {'clip','seq'}, dimensions={0}, use_global_device_ids=true | all-gather | bytes 331776 | tf_op jit(solution)/shard_map/all_gather | solution.py:44
  91.0 16.6 %all_gather.52 = bf16[768,192]{1,0:T(8,128)(2,1)S(1)} all-gather(bf16[96,192]{1,0:T(8,128)(2,1)S(1)} %copy-done.28), channel_id=1, replica_groups=mesh['clip'=4,'seq'=2,'head'=4] {'clip','seq'}, dimensions={0}, use_global_device_ids=true | all-gather | bytes 331776 | tf_op jit(solution)/shard_map/all_gather | solution.py:46
  108.9 9.9 %all-gather.2 = bf16[2,750,192]{1,2,0:T(8,128)(2,1)S(1)} all-gather(bf16[1,750,192]{1,2,0:T(8,128)(2,1)S(1)} %fusion.40), channel_id=2, replica_groups=mesh['clip'=4,'seq'=2,'head'=4] {'seq'}, dimensions={0}, use_global_device_ids=true | all-gather | bytes 864000 | tf_op jit(solution)/shard_map/all_gather | solution.py:135
  123.2 16.6 %all_gather.57 = bf16[192,768]{0,1:T(8,128)(2,1)S(1)} all-gather(bf16[192,96]{0,1:T(8,128)(2,1)S(1)} %copy.40), channel_id=1, replica_groups=mesh['clip'=4,'seq'=2,'head'=4] {'clip','seq'}, dimensions={1}, use_global_device_ids=true | all-gather | bytes 331776 | tf_op jit(solution)/shard_map/all_gather | solution.py:54
  140.4 7.0 %multiply_reduce_fusion.1 = (f32[3,750]{1,0:T(4,128)S(1)}, f32[3,750,1500]{2,1,0:T(8,128)}) fusion(bf16[750,3,64]{0,2,1:T(8,128)(2,1)S(1)} %bitcast.146, bf16[1500,3,64]{0,2,1:T(8,128)(2,1)S(1)} %reshape.253), kind=kOutput, calls=%fused_computation.6 | convolution fusion | flops 438747744 | bytes 14373000 | tf_op jit(solution)/shard_map/while/body/eval_jaxpr/qhd,khd->hqk/dot_general | solution.py:144
  147.4 7.4 %fusion = f32[3,750]{1,0:T(4,128)S(1)} fusion(f32[3,750,1500]{2,1,0:T(8,128)} %get-tuple-element.151, f32[3,750]{1,0:T(4,128)S(1)} %get-tuple-element.150), kind=kLoop, calls=%fused_computation.5 | loop fusion | flops 10122750 | bytes 13518000 | tf_op jit(solution)/shard_map/while/body/eval_jaxpr/reduce_sum | solution.py:149
  154.8 6.6 fusion.38
  164.7 94.1 %all-reduce.23.cloned.1.call-done = f32[750,768]{1,0:T(8,128)} async-done(((f32[750,768]{1,0:T(8,128)}), f32[750,768]{1,0:T(8,128)}) %all-reduce.23.cloned.1.call-update) | async-done | bytes 2304016 | tf_op jit(solution)/shard_map/psum | solution.py:61
  261.2 8.9 %multiply_convert_fusion.1 = (bf16[750,768]{1,0:T(8,128)(2,1)}, f32[750,768]{1,0:T(8,128)}, f32[750,768]{1,0:T(8,128)}) fusion(f32[768]{0:T(1024)S(1)} %convert_element_type.151, bf16[768,768]{1,0:T(8,128)(2,1)} %all-gather.7.cloned.1.call-done, f32[750,768]{1,0:T(8,128)S(1)} %get-tuple-element.147, f32[768]{0:T(1024)S(1)} %convert_element_type.149, ...), kind=kOutput, calls=%fused_computation.48 | convolution fusion | flops 925632000 | bytes 9258864 | tf_op jit(solution)/shard_map/dot_general | solution.py:164
  270.1 4.8 convert_reduce_fusion.2
  280.3 4.1 fusion.71
  284.4 86.5 %all-reduce.25.cloned.1.call-done = f32[750,768]{1,0:T(8,128)} async-done(((f32[750,768]{1,0:T(8,128)}), f32[750,768]{1,0:T(8,128)}) %all-reduce.25.cloned.1.call-update) | async-done | bytes 2304016 | tf_op jit(solution)/shard_map/psum | solution.py:61
  376.9 7.7 %fusion.2 = f32[3,64,1500]{2,1,0:T(8,128)} fusion(bf16[750,3,64]{0,2,1:T(8,128)(2,1)S(1)} %bitcast.144, f32[3,750,1500]{2,1,0:T(8,128)} %get-tuple-element.151, f32[3,750]{1,0:T(4,128)S(1)} %log_add_fusion), kind=kOutput, calls=%fused_computation.8 | convolution fusion | flops 442124992 | bytes 14949000 | tf_op jit(solution)/shard_map/while/body/eval_jaxpr/hqk,qhd->khd/dot_general | solution.py:243
  384.6 7.0 %multiply_reduce_fusion = (f32[3,750]{1,0:T(4,128)S(1)}, f32[3,750,1500]{2,1,0:T(8,128)}) fusion(f32[3,750,1500]{2,1,0:T(8,128)S(1)} %bitcast.141, f32[3,750]{1,0:T(4,128)S(1)} %log_add_fusion, bf16[750,3,64]{0,2,1:T(8,128)(2,1)S(1)} %bitcast.145, bf16[1500,3,64]{0,2,1:T(8,128)(2,1)S(1)} %copy-done.18), kind=kOutput, calls=%fused_computation.1 | convolution fusion | flops 445497760 | bytes 27882000 | tf_op jit(solution)/shard_map/while/body/eval_jaxpr/qhd,khd->hqk/dot_general | solution.py:249
  391.6 6.9 multiply_convert_fusion
  405.2 62.3 %all-reduce.28 = (bf16[1,1500,192]{1,2,0:T(8,128)(2,1)}, bf16[1,1500,192]{1,2,0:T(8,128)(2,1)}) all-reduce(f32[1,1500,192]{1,2,0:T(8,128)} %bitcast.142, f32[1,1500,192]{1,2,0:T(8,128)} %bitcast.143), channel_id=4, replica_groups=mesh['clip'=4,'seq'=2,'head'=4] {'seq'}, use_global_device_ids=true, to_apply=%region_12.13.clone | all-reduce | flops 576000 | bytes 3456000
  481.9 4.2 fusion.61
  486.1 4.2 fusion.43
  494.2 145.7 %all-reduce.27.cloned.1.call-done = (f32[750,768]{1,0:T(8,128)}, f32[750,768]{1,0:T(8,128)}) async-done(((f32[750,768]{1,0:T(8,128)}, f32[750,768]{1,0:T(8,128)}), (f32[750,768]{1,0:T(8,128)}, f32[750,768]{1,0:T(8,128)})) %all-reduce.27.cloned.1.call-update) | async-done | bytes 4608016 | tf_op jit(solution)/shard_map/psum | solution.py:61
  642.5 25.1 %all-reduce.14 = (f32[768]{0:T(1024)S(1)}, f32[768]{0:T(1024)S(1)}, f32[192]{0:T(256)}, f32[192]{0:T(256)}, f32[768]{0:T(1024)S(1)}, /*index=5*/f32[768]{0:T(102...) all-reduce(f32[768]{0:T(1024)S(1)} %get-tuple-element.115, ...), channel_id=6, replica_groups=mesh['clip'=4,'seq'=2,'head'=4] {'clip','seq'}, use_global_device_ids=true, to_apply=%region_18.19.clone | all-reduce | flops 5760 | bytes 46080
  673.9 3.8 copy.41
  (183 shorter events, 72.3 us)
Async XLA Ops:
  8.0 52.0 %copy-start = (bf16[1,750,768]{2,1,0:T(8,128)(2,1)S(1)}, bf16[1,750,768]{2,1,0:T(8,128)(2,1)}, u32[]{:S(2)}) copy-start(bf16[1,750,768]{2,1,0:T(8,128)(2,1)} %param.17) | copy-start | bytes 3456004
  8.0 36.0 %copy-start.26 = (bf16[96,192]{1,0:T(8,128)(2,1)S(1)}, bf16[96,192]{1,0:T(8,128)(2,1)}, u32[]{:S(2)}) copy-start(bf16[96,192]{1,0:T(8,128)(2,1)} %param.22) | copy-start | bytes 110596
  8.0 250.7 %all-reduce.23.cloned.1.call-start = ((), (), s32[]{:S(2)}) async-start(), calls=%async_computation.6 | async-start | bytes 4620288 | tf_op jit(solution)/shard_map/psum | solution.py:61
  60.0 11.6 %copy-start.8 = (bf16[768,192]{1,0:T(8,128)(2,1)}, bf16[768,192]{1,0:T(8,128)(2,1)S(1)}, u32[]{:S(2)}) copy-start(bf16[768,192]{1,0:T(8,128)(2,1)S(1)} %all_gather.55) | copy-start | bytes 884740
  60.5 14.8 %copy-start.27 = (bf16[96,192]{1,0:T(8,128)(2,1)S(1)}, bf16[96,192]{1,0:T(8,128)(2,1)}, u32[]{:S(2)}) copy-start(bf16[96,192]{1,0:T(8,128)(2,1)} %param.20) | copy-start | bytes 110596
  60.5 30.5 %copy-start.32 = (bf16[192]{0:T(256)(128)(2,1)S(1)}, bf16[192]{0:T(256)(128)(2,1)}, u32[]{:S(2)}) copy-start(bf16[192]{0:T(256)(128)(2,1)} %param.21) | copy-start | bytes 1156
  60.5 30.5 %copy-start.28 = (bf16[96,192]{1,0:T(8,128)(2,1)S(1)}, bf16[96,192]{1,0:T(8,128)(2,1)}, u32[]{:S(2)}) copy-start(bf16[96,192]{1,0:T(8,128)(2,1)} %param.23) | copy-start | bytes 110596
  61.1 46.5 %copy-start.33 = (bf16[192]{0:T(256)(128)(2,1)S(1)}, bf16[192]{0:T(256)(128)(2,1)}, u32[]{:S(2)}) copy-start(bf16[192]{0:T(256)(128)(2,1)} %param.24) | copy-start | bytes 1156
  75.3 65.1 %copy-start.5 = (bf16[1500,3,64]{0,2,1:T(8,128)(2,1)}, bf16[1500,3,64]{0,2,1:T(8,128)(2,1)S(1)}, u32[]{:S(2)}) copy-start(bf16[1500,3,64]{0,2,1:T(8,128)(2,1)S(1)} %reshape.253) | copy-start | bytes 1728004
  91.0 48.8 %copy-start.9 = (bf16[768,192]{1,0:T(8,128)(2,1)}, bf16[768,192]{1,0:T(8,128)(2,1)S(1)}, u32[]{:S(2)}) copy-start(bf16[768,192]{1,0:T(8,128)(2,1)S(1)} %all_gather.54) | copy-start | bytes 884740
  108.4 14.7 %copy-start.29 = (bf16[192,96]{1,0:T(8,128)(2,1)S(1)}, bf16[192,96]{1,0:T(8,128)(2,1)}, u32[]{:S(2)}) copy-start(bf16[192,96]{1,0:T(8,128)(2,1)} %param.25) | copy-start | bytes 110596
  139.8 21.6 %copy-start.11 = (bf16[192,768]{0,1:T(8,128)(2,1)}, bf16[192,768]{0,1:T(8,128)(2,1)S(1)}, u32[]{:S(2)}) copy-start(bf16[192,768]{0,1:T(8,128)(2,1)S(1)} %all_gather.57) | copy-start | bytes 884740
  163.4 97.8 %all-gather.7.cloned.1.call-start = ((), (), s32[]{:S(2)}) async-start(), calls=%async_computation.7 | async-start | bytes 1327104 | tf_op jit(solution)/shard_map/all_gather | solution.py:50
  164.0 106.1 %all-gather.9.cloned.1.call-start = ((), (), s32[]{:S(2)}) async-start(), calls=%async_computation.8 | async-start | bytes 1327104 | tf_op jit(solution)/shard_map/all_gather | solution.py:55
  164.6 206.4 %all-reduce.25.cloned.1.call-start = ((), (), s32[]{:S(2)}) async-start(), calls=%async_computation.9 | async-start | bytes 4620288 | tf_op jit(solution)/shard_map/psum | solution.py:61
  278.4 214.1 %reduce-scatter.21.cloned.1.call-start = ((), (), s32[]{:S(2)}) async-start(), calls=%async_computation.15 | async-start | bytes 884736
  373.8 10.8 %slice-start = ((s8[13860864]{0:T(1024)(128)(4,1)}), s8[4194304]{0:T(1024)(128)(4,1)S(1)}, s32[]{:S(2)}) async-start(s8[13860864]{0:T(1024)(128)(4,1)} %bitcast.140), calls=%async_computation.17 | async-start | bytes 8388608
  373.8 10.8 %slice-start.1 = ((s8[13860864]{0:T(1024)(128)(4,1)}), s8[4194304]{0:T(1024)(128)(4,1)S(1)}, s32[]{:S(2)}) async-start(s8[13860864]{0:T(1024)(128)(4,1)} %bitcast.140), calls=%async_computation.18 | async-start | bytes 8388608
  405.2 234.7 %all-reduce.27.cloned.1.call-start = ((), (), s32[]{:S(2)}) async-start(), calls=%async_computation.16 | async-start | bytes 9240576 | tf_op jit(solution)/shard_map/psum | solution.py:61
  472.4 206.7 %reduce-scatter.15.cloned.1.call-start = ((), (), s32[]{:S(2)}) async-start(), calls=%async_computation.12 | async-start | bytes 884736 | tf_op jit(solution)/shard_map/reduce_scatter | solution.py:310
  475.6 203.5 %reduce-scatter.13.cloned.1.call-start = ((), (), s32[]{:S(2)}) async-start(), calls=%async_computation.11 | async-start | bytes 884736 | tf_op jit(solution)/shard_map/reduce_scatter | solution.py:309
  479.0 200.0 %reduce-scatter.11.cloned.1.call-start = ((), (), s32[]{:S(2)}) async-start(), calls=%async_computation.10 | async-start | bytes 884736 | tf_op jit(solution)/shard_map/reduce_scatter | solution.py:308
  481.8 197.3 %reduce-scatter.17.cloned.1.call-start = ((), (), s32[]{:S(2)}) async-start(), calls=%async_computation.13 | async-start | bytes 2654208 | tf_op jit(solution)/shard_map/reduce_scatter | solution.py:314
  486.1 194.0 %reduce-scatter.19.cloned.1.call-start = ((), (), s32[]{:S(2)}) async-start(), calls=%async_computation.14 | async-start | bytes 2654208 | tf_op jit(solution)/shard_map/reduce_scatter | solution.py:319
  (27 other events, 92.8 us)
Sparse Core Ops, SparseCore 0:
  163.5 95.1 all-reduce.22
  278.5 92.3 all-reduce.24
  472.5 167.2 all-reduce.26
Sparse Core Ops, SparseCore 1:
  165.8 25.6 all-gather.6
  193.2 23.8 all-gather.8
  405.3 36.4 reduce-scatter.20
  476.9 33.4 reduce-scatter.14
  514.1 34.9 reduce-scatter.12
  552.8 34.9 reduce-scatter.10
  591.5 42.2 reduce-scatter.16
  637.6 42.4 reduce-scatter.18
where the time goes:
time: 695 us; the launch traced here: 687 us
  waiting for transfers between devices  328 us (47%)
  blocking collectives  198 us (28%)
  matrix products  79.4 us (11%)
  other arithmetic  33.5 us (5%)
  local copies, waits for them, and re-layouts  28.8 us (4%)
  between operations  18.1 us (3%)
    psum x3, waiting for transfers between devices, head_total(): return lax.psum(partial_sum, 'head')  326 us
    unnamed x3, blocking collectives  113 us
    unnamed x103, local copies, waits for them, and re-layouts  20.8 us
    all_gather x1, blocking collectives, fetch_weights(): lax.all_gather(w_value, ('clip', 'seq'), axis=0, tiled=True)  16.6 us
    all_gather x1, blocking collectives, fetch_weights(): lax.all_gather(w_out, ('clip', 'seq'), axis=1, tiled=True)  16.6 us
    all_gather x1, blocking collectives, fetch_weights(): lax.all_gather(w_key, ('clip', 'seq'), axis=0, tiled=True)  15.9 us
    all_gather x1, blocking collectives, fetch_weights(): lax.all_gather(w_query, ('clip', 'seq'), axis=0, tiled=True)  15.6 us
  transfers between devices with their start and end apart: 11, of which 4 were waited for; matrix products, arithmetic and copies ran while one was open for 8% of the time, Pallas kernels for 0%

commit v1 on v0

--- a/solution.py
+++ b/solution.py
@@ -6,6 +6,18 @@
 
 HEAD_DIM = 64
 eps = 1e-05
+
+
+def collect(value, axis, dim):
+    ways, here = (lax.axis_size(axis), lax.axis_index(axis))
+    grown, reach = (value, 1)
+    while reach < ways:
+        theirs = lax.ppermute(grown, axis, [(d, d ^ reach) for d in range(ways)])
+        mine_first = jnp.concatenate([grown, theirs], axis=dim)
+        theirs_first = jnp.concatenate([theirs, grown], axis=dim)
+        grown = jnp.where(here & reach == 0, mine_first, theirs_first)
+        reach = 2 * reach
+    return grown
 
 
 def layer_norm_forward(values, norm_gain, norm_shift):
@@ -41,7 +53,7 @@
     rows = (
         lax.all_gather(gain_one, ("clip", "seq"), axis=0, tiled=True),
         lax.all_gather(shift_one, ("clip", "seq"), axis=0, tiled=True),
-        lax.all_gather(w_query, ("clip", "seq"), axis=0, tiled=True),
+        collect(w_query, ("clip", "seq"), 0),
         lax.all_gather(w_key, ("clip", "seq"), axis=0, tiled=True),
         lax.all_gather(w_value, ("clip", "seq"), axis=0, tiled=True),
         lax.all_gather(b_out, ("clip", "seq"), axis=0, tiled=True),

time: 695 us -> 716 us (1.030)
  waiting for transfers between devices: 328 us -> 352 us
  blocking collectives: 198 us -> 175 us
  matrix products: 79.4 us -> 90.1 us
    reduce_scatter x1, waiting for transfers between devices: 0.97 us -> 26 us  [on_device(): lax.psum_scatter(grad_w_fc_two, ('clip', 'seq'), scatter_dimension=1, til...]
    all_gather x1 -> x0, blocking collectives: 15.6 us -> none  [fetch_weights(): lax.all_gather(w_query, ('clip', 'seq'), axis=0, tiled=True)]
  transfers between devices with their start and end apart: 11 -> 14, of which waited for: 4 -> 5; matrix products, arithmetic and copies ran while one was open for 8% -> 11% of each run, Pallas kernels for 0% -> 0%
where the time goes in v1:
time: 716 us; the launch traced here: 709 us
  waiting for transfers between devices  352 us (49%)
  blocking collectives  175 us (24%)
  matrix products  90.1 us (13%)
  other arithmetic  37.9 us (5%)
  local copies, waits for them, and re-layouts  30.3 us (4%)
  between operations  18.1 us (3%)
    psum x3, waiting for transfers between devices, head_total(): return lax.psum(partial_sum, 'head')  321 us
    unnamed x3, blocking collectives  107 us
    reduce_scatter x1, waiting for transfers between devices, on_device(): lax.psum_scatter(grad_w_fc_two, ('clip', 'seq'), scatter_dimension=1, til...  26 us
    unnamed x103, local copies, waits for them, and re-layouts  22.3 us
    all_gather x1, blocking collectives, fetch_weights(): lax.all_gather(w_key, ('clip', 'seq'), axis=0, tiled=True)  17.4 us
    all_gather x1, blocking collectives, fetch_weights(): lax.all_gather(w_out, ('clip', 'seq'), axis=1, tiled=True)  16.4 us
    all_gather x1, blocking collectives, fetch_weights(): lax.all_gather(w_value, ('clip', 'seq'), axis=0, tiled=True)  15.9 us
  transfers between devices with their start and end apart: 14, of which 5 were waited for; matrix products, arithmetic and copies ran while one was open for 11% of the time, Pallas kernels for 0%

profile of v1, /device:TPU:0, one launch (start us, length us, event | category | flops | bytes accessed | tf_op | source)
XLA Modules:
  0.0 709.3 jit_solution(6785153578488940923)
XLA Ops:
  18.2 22.9 %all-reduce.17 = (bf16[768]{0:T(1024)(128)(2,1)S(1)}, bf16[768]{0:T(1024)(128)(2,1)S(1)}, bf16[768]{0:T(1024)(128)(2,1)S(1)}, bf16[768]{0:T(1024)(128)(2,1)S(1)}...) all-reduce(bf16[768]{0:T(1024)(128)(2,1)S(1)} %dynamic-update-slice, ...), channel_id=1, replica_groups=mesh['clip'=4,'seq'=2,'head'=4] {'clip','seq'}, use_global_device_ids=true, to_apply=%add.1 | all-reduce | flops 4608 | bytes 18432
  44.4 17.4 %all_gather.50 = bf16[768,192]{1,0:T(8,128)(2,1)S(1)} all-gather(bf16[96,192]{1,0:T(8,128)(2,1)S(1)} %copy-done.25), channel_id=1, replica_groups=mesh['clip'=4,'seq'=2,'head'=4] {'clip','seq'}, dimensions={0}, use_global_device_ids=true | all-gather | bytes 331776 | tf_op jit(solution)/shard_map/all_gather | solution.py:57
  61.8 15.9 %all_gather.48 = bf16[768,192]{1,0:T(8,128)(2,1)S(1)} all-gather(bf16[96,192]{1,0:T(8,128)(2,1)S(1)} %copy-done.26), channel_id=1, replica_groups=mesh['clip'=4,'seq'=2,'head'=4] {'clip','seq'}, dimensions={0}, use_global_device_ids=true | all-gather | bytes 331776 | tf_op jit(solution)/shard_map/all_gather | solution.py:58
  81.7 9.8 %all-gather.3 = bf16[2,750,192]{1,2,0:T(8,128)(2,1)S(1)} all-gather(bf16[1,750,192]{1,2,0:T(8,128)(2,1)} %fusion.39), channel_id=3, replica_groups=mesh['clip'=4,'seq'=2,'head'=4] {'seq'}, dimensions={0}, use_global_device_ids=true | all-gather | bytes 864000 | tf_op jit(solution)/shard_map/all_gather | solution.py:146
  96.9 8.5 %all-gather.2 = bf16[2,750,192]{1,2,0:T(8,128)(2,1)S(1)} all-gather(bf16[1,750,192]{1,2,0:T(8,128)(2,1)S(1)} %fusion.40), channel_id=2, replica_groups=mesh['clip'=4,'seq'=2,'head'=4] {'seq'}, dimensions={0}, use_global_device_ids=true | all-gather | bytes 864000 | tf_op jit(solution)/shard_map/all_gather | solution.py:147
  109.8 16.4 %all_gather.52 = bf16[192,768]{0,1:T(8,128)(2,1)S(1)} all-gather(bf16[192,96]{0,1:T(8,128)(2,1)S(1)} %copy.40), channel_id=1, replica_groups=mesh['clip'=4,'seq'=2,'head'=4] {'clip','seq'}, dimensions={1}, use_global_device_ids=true | all-gather | bytes 331776 | tf_op jit(solution)/shard_map/all_gather | solution.py:66
  128.1 7.0 multiply_reduce_fusion.1
  135.1 7.4 %fusion = f32[3,750]{1,0:T(4,128)S(1)} fusion(f32[3,750,1500]{2,1,0:T(8,128)} %get-tuple-element.151, f32[3,750]{1,0:T(4,128)S(1)} %get-tuple-element.150), kind=kLoop, calls=%fused_computation.5 | loop fusion | flops 10122750 | bytes 13518000 | tf_op jit(solution)/shard_map/while/body/eval_jaxpr/reduce_sum | solution.py:161
  142.5 6.6 fusion.38
  152.4 93.1 %all-reduce.23.cloned.1.call-done = f32[750,768]{1,0:T(8,128)} async-done(((f32[750,768]{1,0:T(8,128)}), f32[750,768]{1,0:T(8,128)}) %all-reduce.23.cloned.1.call-update) | async-done | bytes 2304016 | tf_op jit(solution)/shard_map/psum | solution.py:73
  248.0 8.9 %multiply_convert_fusion.1 = (bf16[750,768]{1,0:T(8,128)(2,1)}, f32[750,768]{1,0:T(8,128)}, f32[750,768]{1,0:T(8,128)}) fusion(f32[768]{0:T(1024)S(1)} %convert_element_type.151, bf16[768,768]{1,0:T(8,128)(2,1)} %all-gather.7.cloned.1.call-done, f32[750,768]{1,0:T(8,128)S(1)} %get-tuple-element.147, f32[768]{0:T(1024)S(1)} %convert_element_type.149, ...), kind=kOutput, calls=%fused_computation.48 | convolution fusion | flops 925632000 | bytes 9258864 | tf_op jit(solution)/shard_map/dot_general | solution.py:176
  256.9 4.8 convert_reduce_fusion.2
  267.1 4.2 fusion.73
  271.3 86.5 %all-reduce.25.cloned.1.call-done = f32[750,768]{1,0:T(8,128)} async-done(((f32[750,768]{1,0:T(8,128)}), f32[750,768]{1,0:T(8,128)}) %all-reduce.25.cloned.1.call-update) | async-done | bytes 2304016 | tf_op jit(solution)/shard_map/psum | solution.py:73
  363.3 12.2 %multiply_reduce_fusion = (f32[3,750]{1,0:T(4,128)S(1)}, f32[3,750,1500]{2,1,0:T(8,128)}) fusion(f32[3,750,1500]{2,1,0:T(8,128)} %get-tuple-element.151, f32[3,750]{1,0:T(4,128)S(1)} %log_add_fusion, bf16[750,3,64]{0,2,1:T(8,128)(2,1)S(1)} %bitcast.142, bf16[1500,3,64]{0,2,1:T(8,128)(2,1)S(1)} %copy-done.15), kind=kOutput, calls=%fused_computation.1 | convolution fusion | flops 445497760 | bytes 27882000 | tf_op jit(solution)/shard_map/while/body/eval_jaxpr/qhd,khd->hqk/dot_general | solution.py:261
  381.3 10.1 %multiply_convert_fusion = bf16[3,750,1500]{2,1,0:T(8,128)(2,1)S(1)} fusion(f32[3,750,1500]{2,1,0:T(8,128)} %get-tuple-element.154, f32[3,750,1500]{2,1,0:T(8,128)} %get-tuple-element.151, f32[3,750]{1,0:T(4,128)S(1)} %get-tuple-element.153, f32[3,750]{1,0:T(4,128)S(1)} %log_add_fusion), kind=kLoop, calls=%fused_computation | loop fusion | flops 16875000 | bytes 33768000 | tf_op jit(solution)/shard_map/while/body/eval_jaxpr/convert_element_type | solution.py:265
  394.5 59.2 %all-reduce.28 = (bf16[1,1500,192]{1,2,0:T(8,128)(2,1)}, bf16[1,1500,192]{1,2,0:T(8,128)(2,1)}) all-reduce(f32[1,1500,192]{1,2,0:T(8,128)} %bitcast.141, f32[1,1500,192]{1,2,0:T(8,128)} %bitcast.140), channel_id=5, replica_groups=mesh['clip'=4,'seq'=2,'head'=4] {'seq'}, use_global_device_ids=true, to_apply=%region_13.14.clone | all-reduce | flops 576000 | bytes 3456000
  460.0 5.5 convert_reduce_fusion.4
  479.0 4.1 fusion.63
  483.2 4.2 fusion.43
  495.1 141.8 %all-reduce.27.cloned.1.call-done = (f32[750,768]{1,0:T(8,128)}, f32[750,768]{1,0:T(8,128)}) async-done(((f32[750,768]{1,0:T(8,128)}, f32[750,768]{1,0:T(8,128)}), (f32[750,768]{1,0:T(8,128)}, f32[750,768]{1,0:T(8,128)})) %all-reduce.27.cloned.1.call-update) | async-done | bytes 4608016 | tf_op jit(solution)/shard_map/psum | solution.py:73
  639.6 24.7 %all-reduce.14 = (f32[768]{0:T(1024)S(1)}, f32[768]{0:T(1024)S(1)}, f32[192]{0:T(256)}, f32[192]{0:T(256)}, f32[768]{0:T(1024)S(1)}, /*index=5*/f32[768]{0:T(102...) all-reduce(f32[768]{0:T(1024)S(1)} %get-tuple-element.115, ...), channel_id=6, replica_groups=mesh['clip'=4,'seq'=2,'head'=4] {'clip','seq'}, use_global_device_ids=true, to_apply=%region_18.19.clone | all-reduce | flops 5760 | bytes 46080
  670.8 3.8 copy.41
  676.0 26.0 %reduce-scatter.19.cloned.1.call-done = f32[768,96]{0,1:T(8,128)} async-done(((f32[768,768]{0,1:T(8,128)}), f32[768,96]{0,1:T(8,128)}) %reduce-scatter.19.cloned.1.call-update) | async-done | bytes 294928 | tf_op jit(solution)/shard_map/reduce_scatter | solution.py:331
  (190 shorter events, 90.2 us)
Async XLA Ops:
  8.0 69.7 %copy-start.1 = (bf16[1,750,768]{2,1,0:T(8,128)(2,1)S(1)}, bf16[1,750,768]{2,1,0:T(8,128)(2,1)}, u32[]{:S(2)}) copy-start(bf16[1,750,768]{2,1,0:T(8,128)(2,1)} %param.17) | copy-start | bytes 3456004
  8.0 36.3 %copy-start.25 = (bf16[96,192]{1,0:T(8,128)(2,1)S(1)}, bf16[96,192]{1,0:T(8,128)(2,1)}, u32[]{:S(2)}) copy-start(bf16[96,192]{1,0:T(8,128)(2,1)} %param.22) | copy-start | bytes 110596
  8.0 53.8 %copy-start.26 = (bf16[96,192]{1,0:T(8,128)(2,1)S(1)}, bf16[96,192]{1,0:T(8,128)(2,1)}, u32[]{:S(2)}) copy-start(bf16[96,192]{1,0:T(8,128)(2,1)} %param.23) | copy-start | bytes 110596
  8.1 69.7 %copy-start.32 = (bf16[192]{0:T(256)(128)(2,1)S(1)}, bf16[192]{0:T(256)(128)(2,1)}, u32[]{:S(2)}) copy-start(bf16[192]{0:T(256)(128)(2,1)} %param.24) | copy-start | bytes 1156
  8.1 237.5 %all-reduce.23.cloned.1.call-start = ((), (), s32[]{:S(2)}) async-start(), calls=%async_computation.6 | async-start | bytes 4620288 | tf_op jit(solution)/shard_map/psum | solution.py:73
  8.1 72.0 %collective-permute-start = (bf16[96,192]{1,0:T(8,128)(2,1)}, bf16[96,192]{1,0:T(8,128)(2,1)S(1)}, u32[]{:S(2)}, u32[]{:S(2)}) collective-permute-start(bf16[96,192]{1,0:T(8,128)(2,1)} %param.20), channel_id=1, source_target_pairs={{0,4},{4,0},{8,12},{12,8},{16,20},{20,16},{24,28},{28,24},{1,5},{5... | collective-permute-start | bytes 110600 | tf_op jit(solution)/shard_map/ppermute | solution.py:15
  61.8 18.3 %copy-start.9 = (bf16[768,192]{1,0:T(8,128)(2,1)}, bf16[768,192]{1,0:T(8,128)(2,1)S(1)}, u32[]{:S(2)}) copy-start(bf16[768,192]{1,0:T(8,128)(2,1)S(1)} %all_gather.50) | copy-start | bytes 884740
  80.2 15.0 %collective-permute-start.1 = (bf16[192,192]{1,0:T(8,128)(2,1)S(1)}, bf16[192,192]{1,0:T(8,128)(2,1)S(1)}, u32[]{:S(2)}, u32[]{:S(2)}) collective-permute-start(bf16[192,192]{1,0:T(8,128)(2,1)S(1)} %maximum_select_fusion.2), channel_id=1, source_target_pairs={{0,8},{4,12},{8,0},{12,4},{16,24},{20,28},{24,16},{28,20},{1,9},{5... | collective-permute-start | bytes 221192 | tf_op jit(solution)/shard_map/ppermute | solution.py:15
  93.0 16.7 %copy-start.27 = (bf16[192,96]{1,0:T(8,128)(2,1)S(1)}, bf16[192,96]{1,0:T(8,128)(2,1)}, u32[]{:S(2)}) copy-start(bf16[192,96]{1,0:T(8,128)(2,1)} %param.25) | copy-start | bytes 110596
  95.2 32.9 %copy-start.7 = (bf16[1500,3,64]{0,2,1:T(8,128)(2,1)}, bf16[1500,3,64]{0,2,1:T(8,128)(2,1)S(1)}, u32[]{:S(2)}) copy-start(bf16[1500,3,64]{0,2,1:T(8,128)(2,1)S(1)} %reshape.253) | copy-start | bytes 1728004
  96.1 30.0 %collective-permute-start.2 = (bf16[384,192]{1,0:T(8,128)(2,1)}, bf16[384,192]{1,0:T(8,128)(2,1)}, u32[]{:S(2)}, u32[]{:S(2)}) collective-permute-start(bf16[384,192]{1,0:T(8,128)(2,1)} %maximum_select_fusion.1), channel_id=1, source_target_pairs={{0,16},{4,20},{8,24},{12,28},{16,0},{20,4},{24,8},{28,12},{1,17},{... | collective-permute-start | bytes 442376 | tf_op jit(solution)/shard_map/ppermute | solution.py:15
  126.2 23.0 %copy-start.12 = (bf16[192,768]{0,1:T(8,128)(2,1)}, bf16[192,768]{0,1:T(8,128)(2,1)S(1)}, u32[]{:S(2)}) copy-start(bf16[192,768]{0,1:T(8,128)(2,1)S(1)} %all_gather.52) | copy-start | bytes 884740
  151.1 96.9 %all-gather.7.cloned.1.call-start = ((), (), s32[]{:S(2)}) async-start(), calls=%async_computation.7 | async-start | bytes 1327104 | tf_op jit(solution)/shard_map/all_gather | solution.py:62
  151.7 105.2 %all-gather.9.cloned.1.call-start = ((), (), s32[]{:S(2)}) async-start(), calls=%async_computation.8 | async-start | bytes 1327104 | tf_op jit(solution)/shard_map/all_gather | solution.py:67
  152.3 205.5 %all-reduce.25.cloned.1.call-start = ((), (), s32[]{:S(2)}) async-start(), calls=%async_computation.9 | async-start | bytes 4620288 | tf_op jit(solution)/shard_map/psum | solution.py:73
  265.3 228.2 %reduce-scatter.21.cloned.1.call-start = ((), (), s32[]{:S(2)}) async-start(), calls=%async_computation.15 | async-start | bytes 884736
  361.8 18.1 %copy-start.2 = (f32[750,768]{1,0:T(8,128)}, f32[750,768]{1,0:T(8,128)S(1)}, u32[]{:S(2)}) copy-start(f32[750,768]{1,0:T(8,128)S(1)} %get-tuple-element.141) | copy-start | bytes 6912004
  361.8 13.7 %slice-start = ((s8[13860864]{0:T(1024)(128)(4,1)}), s8[4194304]{0:T(1024)(128)(4,1)S(1)}, s32[]{:S(2)}) async-start(s8[13860864]{0:T(1024)(128)(4,1)} %bitcast.138), calls=%async_computation.17 | async-start | bytes 8388608
  460.0 177.0 %all-reduce.27.cloned.1.call-start = ((), (), s32[]{:S(2)}) async-start(), calls=%async_computation.16 | async-start | bytes 9240576 | tf_op jit(solution)/shard_map/psum | solution.py:73
  469.5 206.5 %reduce-scatter.11.cloned.1.call-start = ((), (), s32[]{:S(2)}) async-start(), calls=%async_computation.10 | async-start | bytes 884736 | tf_op jit(solution)/shard_map/reduce_scatter | solution.py:320
  472.7 203.2 %reduce-scatter.15.cloned.1.call-start = ((), (), s32[]{:S(2)}) async-start(), calls=%async_computation.12 | async-start | bytes 884736 | tf_op jit(solution)/shard_map/reduce_scatter | solution.py:322
  475.9 200.0 %reduce-scatter.13.cloned.1.call-start = ((), (), s32[]{:S(2)}) async-start(), calls=%async_computation.11 | async-start | bytes 884736 | tf_op jit(solution)/shard_map/reduce_scatter | solution.py:321
  478.9 197.0 %reduce-scatter.17.cloned.1.call-start = ((), (), s32[]{:S(2)}) async-start(), calls=%async_computation.13 | async-start | bytes 2654208 | tf_op jit(solution)/shard_map/reduce_scatter | solution.py:326
  483.1 218.8 %reduce-scatter.19.cloned.1.call-start = ((), (), s32[]{:S(2)}) async-start(), calls=%async_computation.14 | async-start | bytes 2654208 | tf_op jit(solution)/shard_map/reduce_scatter | solution.py:331
  (30 other events, 124.4 us)
Sparse Core Ops, SparseCore 0:
  151.2 94.2 all-reduce.22
  265.4 92.3 all-reduce.24
  469.6 167.2 all-reduce.26
Sparse Core Ops, SparseCore 1:
  153.5 24.7 all-gather.6
  180.0 23.8 all-gather.8
  460.0 33.4 reduce-scatter.20
  497.2 34.9 reduce-scatter.10
  535.9 34.9 reduce-scatter.14
  574.6 34.8 reduce-scatter.12
  613.3 42.5 reduce-scatter.16
  659.6 42.2 reduce-scatter.18
